TPU v7x, 32 devices: a whole 2x2x4 slice. The times are simulated.
32 devices in a mesh: dom: 8 (over z, x), sub: 4 (over y, core).
Axes of the slice: x: 2, y: 2, z: 4, core: 2. Of those that a mesh axis runs over, the one named last changes fastest.
Arguments:
- features: bfloat16 [32768, 256], P(('dom', 'sub')), may hold values from -16 to 16
- weight: bfloat16 [256, 256], replicated, may hold values from -0.375 to 0.375
- send_far: int32 [16384], P(('dom', 'sub')), may hold values from 0 to 1023
- send_near: int32 [4096], P(('dom', 'sub')), may hold values from 0 to 1023
- tile_dst: int32 [512], P(('dom', 'sub')), may hold values from 0 to 7
- inner_src: int32 [256], P(('dom', 'sub')), may hold values from 0 to 7
- outer_src: int32 [256], P(('dom', 'sub')), may hold values from 0 to 4
- tile_live: int32 [32, 2], P(('dom', 'sub')), may hold values from 4 to 8
- tile_weight: bfloat16 [512, 128, 128], P(('dom', 'sub')), may hold values from -0.3125 to 0.3125
Outputs:
- whitened: bfloat16 [32768, 256], P(('dom', 'sub'))
- loss_value: float32 [], replicated
Inputs may be any that keep to these rules, and one draw needn't show every extreme that they name: `send_far`: rows may repeat. `tile_live`: live slots come first in each half of a device's slots.
All inputs are finite; a program needn't handle non-finite values.
Results may differ from a plain program's by a relative error of at most 0.0085.
Values may be sent and summed in bfloat16 or wider, within the bound.
A program may use at most 64 MiB of HBM per device.

v0:
```python
import jax
import jax.numpy as jnp
from jax import lax
from jax.sharding import PartitionSpec as P

epsilon = 1e-05


def aggregate_tiles(slot_weights, source_tiles, dest_tiles, slot_mask, tile_table, local_tiles):
    selected = tile_table[source_tiles]
    products = jnp.einsum(
        "kij,kjf->kif", slot_weights, selected, preferred_element_type=jnp.float32
    )
    tile_index = jnp.arange(local_tiles, dtype=jnp.int32)
    selector = ((dest_tiles[None, :] == tile_index[:, None]) & slot_mask[None, :]).astype(
        jnp.float32
    )
    return jnp.einsum("tk,kif->tif", selector, products, precision=lax.Precision.HIGHEST)


def whiten_map(gram_sum, vertex_count, feat_width):
    identity = jnp.eye(feat_width, dtype=jnp.float32)
    scaled = gram_sum / vertex_count + epsilon * identity
    lower = jnp.linalg.cholesky(scaled)
    inverse = lax.linalg.triangular_solve(lower, identity, left_side=True, lower=True)
    return inverse.T


def apply_whitener(hidden, whitener):
    high_part = whitener.astype(jnp.bfloat16)
    low_part = (whitener - high_part.astype(jnp.float32)).astype(jnp.bfloat16)
    upper_term = jnp.dot(hidden, high_part, preferred_element_type=jnp.float32)
    lower_term = jnp.dot(hidden, low_part, preferred_element_type=jnp.float32)
    return upper_term + lower_term


def body(
    features, weight, send_far, send_near, tile_dst, inner_src, outer_src, tile_live, tile_weight
):
    row_count, feat_width = features.shape
    tile_size = tile_weight.shape[1]
    slot_count = inner_src.shape[0]
    local_tiles = row_count // tile_size
    own_table = features.reshape(local_tiles, tile_size, feat_width)
    slot_index = jnp.arange(slot_count, dtype=jnp.int32)
    inner_mask = slot_index < tile_live[0, 0]
    outer_mask = slot_index < tile_live[0, 1]
    far_rows = lax.all_to_all(features[send_far], "dom", split_axis=0, concat_axis=0, tiled=True)
    near_rows = lax.all_to_all(features[send_near], "sub", split_axis=0, concat_axis=0, tiled=True)
    halo_tiles = jnp.concatenate([far_rows, near_rows], 0).reshape(-1, tile_size, feat_width)
    tile_table = jnp.concatenate([own_table, halo_tiles], 0)
    source_tiles = jnp.concatenate([inner_src, outer_src + local_tiles])
    slot_mask = jnp.concatenate([inner_mask, outer_mask])
    summed = aggregate_tiles(
        tile_weight, source_tiles, tile_dst, slot_mask, tile_table, local_tiles
    )
    aggregate = summed.reshape(row_count, feat_width).astype(jnp.bfloat16)
    projected = jnp.dot(aggregate, weight, preferred_element_type=jnp.float32)
    features_f32 = features.astype(jnp.float32)
    hidden = (features_f32 + jax.nn.silu(projected)).astype(jnp.bfloat16)
    gram_part = lax.dot_general(
        hidden, hidden, (((0,), (0,)), ((), ())), preferred_element_type=jnp.float32
    )
    vertex_count = row_count * lax.axis_size("dom") * lax.axis_size("sub")
    cross_part = lax.dot_general(
        hidden, features, (((0,), (0,)), ((), ())), preferred_element_type=jnp.float32
    )
    square_part = jnp.sum(features_f32 * features_f32)
    gram_sum, cross_sum, square_sum = lax.psum((gram_part, cross_part, square_part), ("dom", "sub"))
    whitener = whiten_map(gram_sum, vertex_count, feat_width)
    white = apply_whitener(hidden, whitener)
    gram_whitened = jnp.dot(gram_sum, whitener, precision=lax.Precision.HIGHEST)
    total_distance = (
        jnp.sum(whitener * gram_whitened) - 2.0 * jnp.sum(whitener * cross_sum) + square_sum
    )
    loss_value = total_distance / (vertex_count * feat_width)
    return (white.astype(jnp.bfloat16), loss_value)


def solution(mesh):
    placed = (
        P(("dom", "sub"), None),
        P(),
        P(("dom", "sub")),
        P(("dom", "sub")),
        P(("dom", "sub")),
        P(("dom", "sub")),
        P(("dom", "sub")),
        P(("dom", "sub"), None),
        P(("dom", "sub"), None, None),
    )
    return jax.shard_map(
        body, mesh=mesh, in_specs=placed, out_specs=(P(("dom", "sub"), None), P()), check_vma=False
    )
```

profile of v0, /device:TPU:0, one launch (start us, length us, event | category | flops | bytes accessed | tf_op | source)
XLA Modules:
  0.0 251.9 jit_solution(10738372148155213875)
XLA Ops:
  7.2 0.7 compare_select_fusion.2
  8.0 2.5 gather_fusion.1
  10.4 4.3 %all-to-all-start.1 = ((bf16[4,32,256]{2,1,0:T(8,128)(2,1)}), bf16[4,32,256]{2,1,0:T(8,128)(2,1)S(1)}, u32[]{:S(2)}, u32[]{:S(2)}) async-start(bf16[4,32,256]{2,1,0:T(8,128)(2,1)} %bitcast.6), calls=%async_computation.1 | async-start | bytes 131072 | tf_op jit(solution)/shard_map/all_to_all | solution.py:49
  14.7 0.7 compare_select_fusion
  15.4 0.7 add_bitcast_fusion
  16.1 2.6 %gather_fusion = bf16[512,256]{1,0:T(8,128)(2,1)} fusion(bf16[1024,256]{1,0:T(8,128)(2,1)S(1)} %copy-done.1, s32[1024]{0:T(1024)S(1)} %pad_clamp_fusion.2), kind=kCustom, calls=%fused_computation | custom fusion | bytes 526336 | tf_op jit(solution)/shard_map/gather | solution.py:48
  18.6 0.2 all-to-all-done.1
  18.8 6.3 %all-to-all-start = ((bf16[8,64,256]{2,1,0:T(8,128)(2,1)}), bf16[8,64,256]{2,1,0:T(8,128)(2,1)S(1)}, u32[]{:S(2)}, u32[]{:S(2)}) async-start(bf16[8,64,256]{2,1,0:T(8,128)(2,1)} %bitcast.4), calls=%async_computation | async-start | bytes 524288 | tf_op jit(solution)/shard_map/all_to_all | solution.py:48
  25.2 0.7 fusion.31
  25.9 1.3 iota_compare_fusion.5
  27.3 7.2 %all-to-all-done = bf16[8,64,256]{2,1,0:T(8,128)(2,1)S(1)} async-done(((bf16[8,64,256]{2,1,0:T(8,128)(2,1)}), bf16[8,64,256]{2,1,0:T(8,128)(2,1)S(1)}, u32[]{:S(2)}, u32[]{:S(2)}) %all-to-all-start) | async-done | bytes 262176 | tf_op jit(solution)/shard_map/all_to_all | solution.py:48
  34.6 1.6 gather_fusion.2
  36.2 1.7 fusion.32
  37.9 2.1 copy.28
  40.0 2.4 fusion.2
  42.4 0.1 copy.19
  42.6 1.1 fusion.7
  43.7 1.0 fusion.33
  44.7 1.0 fusion.34
  45.9 39.3 %psum.23 = f32[]{:T(128)} all-reduce(f32[]{:T(128)} %get-tuple-element.30), channel_id=1, replica_groups=mesh['dom'=8,'sub'=4] {'dom','sub'}, use_global_device_ids=true, to_apply=%region_9.10 | all-reduce | flops 1 | bytes 8 | tf_op jit(solution)/shard_map/psum | solution.py:69
  85.2 89.4 %all-reduce.4.cloned.1.call-done = (f32[256,256]{0,1:T(8,128)}, f32[256,256]{0,1:T(8,128)}) async-done(((f32[256,256]{0,1:T(8,128)}, f32[256,256]{0,1:T(8,128)}), (f32[256,256]{0,1:T(8,128)}, f32[256,256]{0,1:T(8,128)})) %all-reduce.4.cloned.1.call-update) | async-done | bytes 524304 | tf_op jit(solution)/shard_map/psum | solution.py:69
  174.6 1.0 select_add_fusion
  175.6 0.1 copy.21
  175.7 1.0 fusion.11
  176.7 11.7 %cholesky.49 = f32[128,128]{1,0:T(8,128)S(1)} custom-call(f32[128,128]{1,0:T(8,128)S(1)} %cholesky.115), custom_call_target="Cholesky" | custom-call | tf_op jit(solution)/shard_map/jit(cholesky)/cholesky | solution.py:24
  188.4 0.1 copy.22
  188.6 9.8 %custom-call.14 = f32[1,128,128]{1,2,0:T(8,128)S(1)} custom-call(f32[1,128,128]{2,1,0:T(8,128)S(1)} %get-tuple-element.33), custom_call_target="InvertDiagBlocksLowerTriangular" | custom-call | tf_op jit(solution)/shard_map/jit(cholesky)/cholesky | solution.py:24
  198.4 0.2 fusion.18
  198.7 0.3 convolution_subtract_fusion.1
  199.0 11.7 %cholesky.103 = f32[128,128]{1,0:T(8,128)S(1)} custom-call(f32[128,128]{1,0:T(8,128)S(1)} %convolution_subtract_fusion.1), custom_call_target="Cholesky" | custom-call | tf_op jit(solution)/shard_map/jit(cholesky)/cholesky | solution.py:24
  210.7 0.1 copy.24
  210.8 0.6 compare_reduce_fusion.1
  211.5 0.6 compare_reduce_fusion
  213.6 4.2 %while.1 = (s32[]{:T(128)}, f32[256,256]{0,1:T(8,128)S(1)}, s32[2,2]{1,0:T(2,128)S(1)}, f32[2,128,128]{2,1,0:T(8,128)S(1)}, s32[]{:T(128)}) while((s32[]{:T(128)}, f32[256,256]{0,1:T(8,128)S(1)}, s32[2,2]{1,0:T(2,128)S(1)}, f32[2,128,128]{2,1,0:T(8,128)S(1)}, s32[]{:T(128)}) %tuple.29), condition=%wide.while_cond, body=%wide.while_body.sunk | while | flops 2 | bytes 393329 | solution.py:25
  213.6 0.6 fusion.51
  214.2 1.4 dynamic-slice.7
  215.6 0.1 copy.34
  215.7 0.6 fusion.51
  216.3 1.4 dynamic-slice.7
  217.7 0.1 copy.34
  217.8 19.9 %custom-call.15 = f32[2,128,128]{1,2,0:T(8,128)S(1)} custom-call(f32[2,128,128]{2,1,0:T(8,128)S(1)} %get-tuple-element.9), custom_call_target="InvertDiagBlocksLowerTriangular" | custom-call | tf_op jit(solution)/shard_map/triangular_solve | solution.py:25
  237.7 0.3 fusion.13
  238.0 0.4 convolution_subtract_fusion
  238.4 0.3 fusion.17
  238.7 0.3 fusion.15
  239.0 1.0 fusion.8
  240.0 1.1 fusion.5
  241.2 0.7 fusion.10
  (41 shorter events, 0.7 us)
Async XLA Ops:
  7.2 29.1 %copy-start = (bf16[16,128,128]{2,1,0:T(8,128)(2,1)S(1)}, bf16[16,128,128]{2,1,0:T(8,128)(2,1)}, u32[]{:S(2)}) copy-start(bf16[16,128,128]{2,1,0:T(8,128)(2,1)} %param.17) | copy-start | bytes 1572868
  7.2 8.9 %copy-start.1 = (bf16[1024,256]{1,0:T(8,128)(2,1)S(1)}, bf16[1024,256]{1,0:T(8,128)(2,1)}, u32[]{:S(2)}) copy-start(bf16[1024,256]{1,0:T(8,128)(2,1)} %param.9) | copy-start | bytes 1572868
  7.2 18.0 %copy-start.7 = (s32[8]{0:T(128)S(1)}, s32[8]{0:T(128)}, u32[]{:S(2)}) copy-start(s32[8]{0:T(128)} %param.14) | copy-start | bytes 100
  7.2 18.0 %copy-start.4 = (s32[1,2]{1,0:T(1,128)S(1)}, s32[1,2]{1,0:T(1,128)}, u32[]{:S(2)}) copy-start(s32[1,2]{1,0:T(1,128)} %param.16) | copy-start | bytes 28
  10.4 8.4 %all-to-all-start.1 = ((bf16[4,32,256]{2,1,0:T(8,128)(2,1)}), bf16[4,32,256]{2,1,0:T(8,128)(2,1)S(1)}, u32[]{:S(2)}, u32[]{:S(2)}) async-start(bf16[4,32,256]{2,1,0:T(8,128)(2,1)} %bitcast.6), calls=%async_computation.1 | async-start | bytes 131072 | tf_op jit(solution)/shard_map/all_to_all | solution.py:49
  18.8 15.7 %all-to-all-start = ((bf16[8,64,256]{2,1,0:T(8,128)(2,1)}), bf16[8,64,256]{2,1,0:T(8,128)(2,1)S(1)}, u32[]{:S(2)}, u32[]{:S(2)}) async-start(bf16[8,64,256]{2,1,0:T(8,128)(2,1)} %bitcast.4), calls=%async_computation | async-start | bytes 524288 | tf_op jit(solution)/shard_map/all_to_all | solution.py:48
  25.1 149.5 %all-reduce.4.cloned.1.call-start = ((), (), s32[]{:S(2)}) async-start(), calls=%async_computation.2 | async-start | bytes 1048576 | tf_op jit(solution)/shard_map/psum | solution.py:69
  37.9 2.1 copy-start.5
  40.0 2.6 %copy-start.6 = (bf16[256,256]{1,0:T(8,128)(2,1)S(1)}, bf16[256,256]{1,0:T(8,128)(2,1)}, u32[]{:S(2)}) copy-start(bf16[256,256]{1,0:T(8,128)(2,1)} %param.10) | copy-start | bytes 393220
  213.6 25.5 %copy-start.2 = (f32[256,256]{0,1:T(8,128)S(1)}, f32[256,256]{0,1:T(8,128)}, u32[]{:S(2)}) copy-start(f32[256,256]{0,1:T(8,128)} %get-tuple-element.26) | copy-start | bytes 786436
  238.7 2.5 copy-start.3
Sparse Core Ops, SparseCore 0:
  45.9 128.6 all-reduce.3
where the time goes:
time: 253 us; the launch traced here: 252 us
  waiting for transfers between devices  96.8 us (38%)
  other arithmetic  61 us (24%)
  blocking collectives  39.3 us (16%)
  between operations  18.7 us (7%)
  local copies, waits for them, and re-layouts  14.2 us (6%)
  matrix products  11.3 us (4%)
  starting transfers between devices  10.6 us (4%)
    psum x1, waiting for transfers between devices, body(): lax.psum((gram_part, cross_part, square_part), ('dom', 'sub'))  89.4 us
    psum x1, blocking collectives, body(): lax.psum((gram_part, cross_part, square_part), ('dom', 'sub'))  39.3 us
    another operation x7, other arithmetic, whiten_map(): lower = jnp.linalg.cholesky(scaled)  34.6 us
    another operation x3, other arithmetic, whiten_map(): lax.linalg.triangular_solve(lower, identity, left_side=True, lower=True)  19.9 us
    all_to_all x1, waiting for transfers between devices, body(): lax.all_to_all(features[send_far], 'dom', split_axis=0, concat_axis=0, ti...  7.17 us
    all_to_all x1, starting transfers between devices, body(): lax.all_to_all(features[send_far], 'dom', split_axis=0, concat_axis=0, ti...  6.27 us
  transfers between devices with their start and end apart: 3, of which 3 were waited for; matrix products, arithmetic and copies ran while one was open for 2% of the time, Pallas kernels for 0%

commit v1 on v0

v1 whole, which is shorter than its diff:
```python
import functools

import jax
import jax.numpy as jnp
from jax import lax
from jax.experimental import pallas as pl
from jax.experimental.pallas import tpu as pltpu
from jax.sharding import PartitionSpec as P

epsilon = 1e-05
MESH = pl.DeviceIdType.MESH
LEAF = 64
HIGH = lax.Precision.HIGHEST


def one_hot_rows(index_row, row_count):
    rows = index_row.shape[1]
    columns = jnp.broadcast_to(index_row, (128, rows)).T
    lane = lax.broadcasted_iota(jnp.int32, (rows, 128), 1)
    parts = [
        jnp.where(columns == lane + start, 1.0, 0.0).astype(jnp.bfloat16)
        for start in range(0, row_count, 128)
    ]
    return jnp.concatenate(parts, axis=1)


def padded_rows(count):
    return -(-count // 16) * 16


def packing(packed_rows, padded_total, n_dom, n_sub, per_dom, per_sub, near_rows_each):
    near_total = n_sub * near_rows_each
    far_total = packed_rows - near_total
    far_rows_each = far_total // n_dom
    row = lax.broadcasted_iota(jnp.int32, (packed_rows, padded_total), 0)
    column = lax.broadcasted_iota(jnp.int32, (packed_rows, padded_total), 1)
    far_place = row + lax.div(row, far_rows_each) * (per_dom - far_rows_each)
    near_row = row - far_total
    near_place = (
        n_dom * per_dom + near_row + lax.div(near_row, near_rows_each) * (per_sub - near_rows_each)
    )
    place = jnp.where(row < far_total, far_place, near_place)
    return jnp.where(place == column, 1.0, 0.0).astype(jnp.bfloat16)


def leaf_inverse(block):
    size = block.shape[0]
    row = lax.broadcasted_iota(jnp.int32, (size, size), 0)
    lane = lax.broadcasted_iota(jnp.int32, (size, size), 1)
    work = jnp.concatenate([block, jnp.where(row == lane, 1.0, 0.0)], axis=1)
    wide_row = lax.broadcasted_iota(jnp.int32, (size, 1), 0)
    for step in range(size - 1):
        pivot_row = work[step : step + 1, :]
        scaled = pivot_row * (1.0 / pivot_row[:, step : step + 1])
        column = work[:, step : step + 1]
        work = work - jnp.where(wide_row > step, column, 0.0) * scaled
    diagonal = jnp.sum(jnp.where(row == lane, work[:, :size], 0.0), axis=1, keepdims=True)
    return work[:, size:] * (1.0 / jnp.sqrt(diagonal))


def kernel(
    n_dom,
    n_sub,
    near_each,
    features_ref,
    weight_ref,
    far_ref,
    near_ref,
    dst_ref,
    inner_ref,
    outer_ref,
    live_ref,
    tile_ref,
    out_ref,
    loss_ref,
    far_send,
    near_send,
    arrived,
    table,
    products,
    acc,
    aggregate,
    gram_part,
    cross_part,
    gram_in,
    cross_in,
    gram_own,
    cross_own,
    gram,
    cross,
    work,
    halo_sems,
    sum_sems,
):
    total_devices = n_dom * n_sub
    dom = lax.axis_index("dom")
    sub = lax.axis_index("sub")
    me = dom * n_sub + sub
    tiles, size, feat = features_ref.shape
    rows = tiles * size
    slots = inner_ref.shape[0]
    owners = min(total_devices, feat // 8)
    share = feat // owners
    own_rows = pl.ds(pl.multiple_of(lax.rem(me, owners) * share, share), share)

    def device_of(index):
        return (lax.div(index, n_sub), lax.rem(index, n_sub))

    barrier = pltpu.get_barrier_semaphore()

    @pl.loop(1, total_devices)
    def _(offset):
        peer = lax.rem(me + offset, total_devices)
        pl.semaphore_signal(barrier, inc=1, device_id=device_of(peer), device_id_type=MESH)

    features = features_ref[...].reshape(rows, feat)
    far_rows = jnp.dot(
        one_hot_rows(far_ref[...], rows), features, preferred_element_type=jnp.float32
    ).astype(jnp.bfloat16)
    near_rows = jnp.dot(
        one_hot_rows(near_ref[...], rows), features, preferred_element_type=jnp.float32
    ).astype(jnp.bfloat16)
    far_send[...] = far_rows
    near_send[...] = near_rows
    per_dom = far_send.shape[0] // n_dom
    per_sub = near_send.shape[0] // n_sub
    far_count = per_dom * n_dom
    packed = size % per_dom == 0 and size % per_sub == 0 and arrived.shape[0] == table.shape[0] * size

    def place(first, count):
        if packed:
            within = pl.multiple_of(lax.rem(first, size), count)
            return table.at[lax.div(first, size), pl.ds(within, count)]
        return arrived.at[pl.ds(pl.multiple_of(first, count), count)]

    def dom_rows(index):
        return pl.ds(pl.multiple_of(index * per_dom, per_dom), per_dom)

    def sub_rows(index):
        return pl.ds(pl.multiple_of(index * per_sub, per_sub), per_sub)

    def dom_place(index):
        return place(index * per_dom, per_dom)

    def sub_place(index):
        return place(far_count + index * per_sub, per_sub)

    pl.semaphore_wait(barrier, total_devices - 1)

    @pl.loop(1, n_dom)
    def _(offset):
        peer = lax.rem(dom + offset, n_dom)
        pltpu.make_async_remote_copy(
            src_ref=far_send.at[dom_rows(peer)],
            dst_ref=dom_place(dom),
            send_sem=halo_sems.at[0],
            recv_sem=halo_sems.at[1],
            device_id=(peer, sub),
            device_id_type=MESH,
        ).start()

    @pl.loop(1, n_sub)
    def _(offset):
        peer = lax.rem(sub + offset, n_sub)
        pltpu.make_async_remote_copy(
            src_ref=near_send.at[sub_rows(peer)],
            dst_ref=sub_place(sub),
            send_sem=halo_sems.at[2],
            recv_sem=halo_sems.at[3],
            device_id=(dom, peer),
            device_id_type=MESH,
        ).start()

    dom_place(dom)[...] = far_send[dom_rows(dom), :]
    sub_place(sub)[...] = near_send[sub_rows(sub), :]

    def slot_products(rows_ref, source, first):
        for slot in range(slots):
            products[slot] = jnp.dot(
                tile_ref[first + slot],
                rows_ref[source[slot]],
                preferred_element_type=jnp.float32,
            )

    def slot_sum(tile, first, count):
        total = None
        for slot in range(slots):
            target = jnp.full((1, feat), dst_ref[first + slot], jnp.int32)
            chosen = jnp.where(jnp.logical_and(target == tile, count > slot), 1.0, 0.0)
            term = products[slot] * chosen
            total = term if total is None else total + term
        return total

    slot_products(features_ref, inner_ref, 0)
    inner_count = jnp.full((1, feat), live_ref[0, 0], jnp.int32)
    outer_count = jnp.full((1, feat), live_ref[0, 1], jnp.int32)

    @pl.loop(0, tiles)
    def _(tile):
        acc[tile] = slot_sum(tile, 0, inner_count)

    features_t = features.T
    wide = features.astype(jnp.float32)
    square = jnp.sum(wide * wide)
    cross_part[:, feat:] = jnp.broadcast_to(square, (feat, cross_part.shape[1] - feat))

    def settle(ref, sem):
        pltpu.make_async_copy(ref, ref, sem).wait()

    settle(arrived.at[pl.ds(0, per_dom * (n_dom - 1))], halo_sems.at[1])
    settle(arrived.at[pl.ds(0, per_sub * (n_sub - 1))], halo_sems.at[3])
    if not packed:
        table[...] = jnp.dot(
            packing(table.shape[0] * size, arrived.shape[0], n_dom, n_sub, per_dom, per_sub, near_each),
            arrived[...],
            preferred_element_type=jnp.float32,
        ).astype(jnp.bfloat16).reshape(table.shape)
    slot_products(table, outer_ref, slots)

    @pl.loop(0, tiles)
    def _(tile):
        total = acc[tile] + slot_sum(tile, slots, outer_count)
        aggregate[pl.ds(pl.multiple_of(tile * size, size), size), :] = total.astype(jnp.bfloat16)

    projected = jnp.dot(aggregate[...], weight_ref[...], preferred_element_type=jnp.float32)
    hidden = (
        features_ref[...].reshape(rows, feat).astype(jnp.float32) + projected / (1.0 + jnp.exp(-projected))
    ).astype(jnp.bfloat16)
    gram_part[...] = jnp.dot(hidden.T, hidden, preferred_element_type=jnp.float32)

    def scatter(part, landing, first):
        def send(offset):
            peer = lax.rem(me + offset, total_devices)

            def go():
                pltpu.make_async_remote_copy(
                    src_ref=part.at[pl.ds(pl.multiple_of(peer * share, share), share)],
                    dst_ref=landing.at[me],
                    send_sem=sum_sems.at[first],
                    recv_sem=sum_sems.at[first + 1],
                    device_id=device_of(peer),
                    device_id_type=MESH,
                ).start()

            if owners == total_devices:
                go()
            else:
                pl.when(peer < owners)(go)

        pl.loop(1, total_devices)(send)

    def reduce_and_gather(part, landing, own, full, first):
        def go():
            landing[me] = part[own_rows, :]
            settle(landing.at[pl.ds(0, total_devices - 1)], sum_sems.at[first + 1])
            total = jnp.sum(landing[...], axis=0)
            own[...] = total
            full[own_rows, :] = total

            @pl.loop(1, total_devices)
            def _(offset):
                peer = lax.rem(me + offset, total_devices)
                pltpu.make_async_remote_copy(
                    src_ref=own,
                    dst_ref=full.at[own_rows],
                    send_sem=sum_sems.at[first + 2],
                    recv_sem=sum_sems.at[first + 3],
                    device_id=device_of(peer),
                    device_id_type=MESH,
                ).start()

        if owners == total_devices:
            go()
        else:
            pl.when(me < owners)(go)

    def finish(part, landing, full, first):
        def owner():
            settle(full.at[pl.ds(0, share * (owners - 1))], sum_sems.at[first + 3])

        def other():
            settle(full, sum_sems.at[first + 3])

        if owners == total_devices:
            owner()
        else:
            pl.when(me < owners)(owner)
            pl.when(me >= owners)(other)

    def drain(part, landing, first):
        def owner():
            settle(part.at[pl.ds(0, share * (owners - 1))], sum_sems.at[first])
            settle(landing.at[pl.ds(0, total_devices - 1)], sum_sems.at[first + 2])

        def other():
            settle(part, sum_sems.at[first])

        if owners == total_devices:
            owner()
        else:
            pl.when(me < owners)(owner)
            pl.when(me >= owners)(other)

    scatter(gram_part, gram_in, 0)
    cross_part[:, :feat] = jnp.dot(features_t, hidden, preferred_element_type=jnp.float32)
    reduce_and_gather(gram_part, gram_in, gram_own, gram, 0)
    scatter(cross_part, cross_in, 4)
    finish(gram_part, gram_in, gram, 0)

    vertex_count = rows * total_devices
    diagonal = lax.broadcasted_iota(jnp.int32, (feat, feat), 0) == lax.broadcasted_iota(
        jnp.int32, (feat, feat), 1
    )
    identity = jnp.where(diagonal, 1.0, 0.0)
    work[:, :feat] = gram[...] / vertex_count + epsilon * identity
    work[:, feat:] = identity
    for start in range(0, feat, LEAF):
        stop = start + LEAF
        inverse = leaf_inverse(work[start:stop, start:stop])
        pivot_rows = jnp.dot(
            inverse, work[start:stop, :], precision=HIGH, preferred_element_type=jnp.float32
        )
        work[start:stop, :] = pivot_rows
        if stop < feat:
            work[stop:, :] = work[stop:, :] - lax.dot_general(
                pivot_rows[:, stop:feat],
                pivot_rows,
                (((0,), (0,)), ((), ())),
                precision=HIGH,
                preferred_element_type=jnp.float32,
            )
        if start == LEAF:
            reduce_and_gather(cross_part, cross_in, cross_own, cross, 4)

    lower_inverse = work[:, feat:]
    high_part = lower_inverse.astype(jnp.bfloat16)
    low_part = (lower_inverse - high_part.astype(jnp.float32)).astype(jnp.bfloat16)
    across = (((1,), (1,)), ((), ()))
    white = lax.dot_general(
        hidden, high_part, across, preferred_element_type=jnp.float32
    ) + lax.dot_general(hidden, low_part, across, preferred_element_type=jnp.float32)
    out_ref[...] = white.astype(jnp.bfloat16)

    whitened_gram = jnp.dot(
        lower_inverse, gram[...], precision=HIGH, preferred_element_type=jnp.float32
    )
    finish(cross_part, cross_in, cross, 4)
    distance = jnp.sum(lower_inverse * (whitened_gram - 2.0 * cross[:, :feat]))
    square_sum = jnp.max(cross[0:8, feat:])
    loss_ref[0, 0] = (distance + square_sum) / (vertex_count * feat)

    settle(far_send.at[pl.ds(0, per_dom * (n_dom - 1))], halo_sems.at[0])
    settle(near_send.at[pl.ds(0, per_sub * (n_sub - 1))], halo_sems.at[2])
    drain(gram_part, gram_in, 0)
    drain(cross_part, cross_in, 4)


def body(
    n_dom,
    n_sub,
    features,
    weight,
    send_far,
    send_near,
    tile_dst,
    inner_src,
    outer_src,
    tile_live,
    tile_weight,
):
    rows, feat = features.shape
    size = tile_weight.shape[1]
    slots = inner_src.shape[0]
    total = n_dom * n_sub
    share = feat // min(total, feat // 8)
    far_count = send_far.shape[0]
    near_count = send_near.shape[0]

    def padded(index, peers):
        each = index.shape[0] // peers
        grid = index.reshape(peers, each)
        return jnp.pad(grid, ((0, 0), (0, padded_rows(each) - each))).reshape(1, -1)

    far_index = padded(send_far, n_dom)
    near_index = padded(send_near, n_sub)
    far_padded = far_index.shape[1]
    near_padded = near_index.shape[1]
    vmem = pl.BlockSpec(memory_space=pltpu.VMEM)
    smem = pl.BlockSpec(memory_space=pltpu.SMEM)
    f32 = jnp.float32
    bf16 = jnp.bfloat16
    cross_width = feat + 128
    whitened, loss = pl.pallas_call(
        functools.partial(kernel, n_dom, n_sub, near_count // n_sub),
        out_shape=(
            jax.ShapeDtypeStruct((rows, feat), bf16),
            jax.ShapeDtypeStruct((1, 1), f32),
        ),
        in_specs=[vmem, vmem, vmem, vmem, smem, smem, smem, smem, vmem],
        out_specs=(vmem, smem),
        scratch_shapes=[
            pltpu.VMEM((far_padded, feat), bf16),
            pltpu.VMEM((near_padded, feat), bf16),
            pltpu.VMEM((far_padded + near_padded, feat), bf16),
            pltpu.VMEM(((far_count + near_count) // size, size, feat), bf16),
            pltpu.VMEM((slots, size, feat), f32),
            pltpu.VMEM((rows // size, size, feat), f32),
            pltpu.VMEM((rows, feat), bf16),
            pltpu.VMEM((feat, feat), f32),
            pltpu.VMEM((feat, cross_width), f32),
            pltpu.VMEM((total, share, feat), f32),
            pltpu.VMEM((total, share, cross_width), f32),
            pltpu.VMEM((share, feat), f32),
            pltpu.VMEM((share, cross_width), f32),
            pltpu.VMEM((feat, feat), f32),
            pltpu.VMEM((feat, cross_width), f32),
            pltpu.VMEM((feat, 2 * feat), f32),
            pltpu.SemaphoreType.DMA((4,)),
            pltpu.SemaphoreType.DMA((8,)),
        ],
        compiler_params=pltpu.CompilerParams(collective_id=0, has_side_effects=True),
    )(
        features.reshape(rows // size, size, feat),
        weight,
        far_index,
        near_index,
        tile_dst,
        inner_src,
        outer_src,
        tile_live,
        tile_weight,
    )
    return whitened, loss.reshape(())


def solution(mesh):
    placed = (
        P(("dom", "sub"), None),
        P(),
        P(("dom", "sub")),
        P(("dom", "sub")),
        P(("dom", "sub")),
        P(("dom", "sub")),
        P(("dom", "sub")),
        P(("dom", "sub"), None),
        P(("dom", "sub"), None, None),
    )
    return jax.shard_map(
        functools.partial(body, mesh.shape["dom"], mesh.shape["sub"]),
        mesh=mesh,
        in_specs=placed,
        out_specs=(P(("dom", "sub"), None), P()),
        check_vma=False,
    )
```

time: 253 us -> 63.7 us (0.25)
  the two profiles are of different devices: /device:TPU:0 before, /device:TPU:31 now
where the time goes in v1:
time: 63.7 us; the launch traced here: 63.5 us
  Pallas kernels  59.3 us (93%)
  between operations  2.34 us (4%)
  local copies, waits for them, and re-layouts  1.87 us (3%)
    pallas_call x1, Pallas kernels, body(): pl.pallas_call(functools.partial(kernel, n_dom, n_sub, near_count // n_su...  59.3 us
    unnamed x1, local copies, waits for them, and re-layouts  1.87 us

profile of v1, /device:TPU:31, one launch (start us, length us, event | category | flops | bytes accessed | tf_op | source)
XLA Modules:
  0.0 63.5 jit_solution(16314685181245920832)
XLA Ops:
  0.6 59.3 %shard_map.104 = (bf16[1024,256]{1,0:T(8,128)(2,1)}, f32[1,1]{1,0:T(1,128)}) custom-call(bf16[8,128,256]{2,1,0:T(8,128)(2,1)} %bitcast.4, bf16[256,256]{1,0:T(8,128)(2,1)} %weight_ref.1, s32[1,512]{1,0:T(1,128)} %bitcast.5, s32[1,128]{1,0:T(1,128)} %bitcast.6, s32[16]{0:T(128)} %dst_ref.1, s32[8]{0:T(128)} %inner_ref.1, s32[8]{0:T(128)} %outer_ref.1, ...), custom_call_target="tpu_custom_call" | custom-call | tf_op jit(solution)/shard_map/pallas_call | solution.py:393
  59.9 1.9 %copy.13 = bf16[1024,256]{1,0:T(8,128)(2,1)} copy(bf16[1024,256]{1,0:T(8,128)(2,1)} %get-tuple-element.8) | data formatting | bytes 1048576

commit v2 on v1

--- a/solution.py
+++ b/solution.py
@@ -48,12 +48,29 @@
     row = lax.broadcasted_iota(jnp.int32, (size, size), 0)
     lane = lax.broadcasted_iota(jnp.int32, (size, size), 1)
     work = jnp.concatenate([block, jnp.where(row == lane, 1.0, 0.0)], axis=1)
-    wide_row = lax.broadcasted_iota(jnp.int32, (size, 1), 0)
-    for step in range(size - 1):
-        pivot_row = work[step : step + 1, :]
-        scaled = pivot_row * (1.0 / pivot_row[:, step : step + 1])
-        column = work[:, step : step + 1]
-        work = work - jnp.where(wide_row > step, column, 0.0) * scaled
+    tall = lax.broadcasted_iota(jnp.int32, (size, 1), 0)
+    for step in range(0, size - 2, 2):
+        first = work[step : step + 1, :]
+        second = work[step + 1 : step + 2, :]
+        a = first[:, step : step + 1]
+        b = first[:, step + 1 : step + 2]
+        c = second[:, step + 1 : step + 2]
+        scale = 1.0 / (a * c - b * b)
+        upper = (c * first - b * second) * scale
+        lower = (a * second - b * first) * scale
+        below = tall > step + 1
+        work = (
+            work
+            - jnp.where(below, work[:, step : step + 1], 0.0) * upper
+            - jnp.where(below, work[:, step + 1 : step + 2], 0.0) * lower
+        )
+    left = work[:, :size]
+    diagonal = jnp.sum(jnp.where(row == lane, left, 0.0), axis=1, keepdims=True)
+    before = jnp.sum(jnp.where(row == lane + 1, left, 0.0), axis=1, keepdims=True)
+    odd = lax.rem(tall, 2) == 1
+    above = pltpu.roll(jnp.broadcast_to(diagonal, (size, 2 * size)), 1, 0)
+    factor = jnp.where(odd, before, 0.0) / above
+    work = work - factor * pltpu.roll(work, 1, 0)
     diagonal = jnp.sum(jnp.where(row == lane, work[:, :size], 0.0), axis=1, keepdims=True)
     return work[:, size:] * (1.0 / jnp.sqrt(diagonal))
 
@@ -62,6 +79,17 @@
     n_dom,
     n_sub,
     near_each,
+    features_in,
+    weight_in,
+    far_in,
+    near_in,
+    dst_in,
+    inner_in,
+    outer_in,
+    live_in,
+    tile_in,
+    out_ref,
+    loss_ref,
     features_ref,
     weight_ref,
     far_ref,
@@ -71,8 +99,7 @@
     outer_ref,
     live_ref,
     tile_ref,
-    out_ref,
-    loss_ref,
+    result,
     far_send,
     near_send,
     arrived,
@@ -81,14 +108,13 @@
     acc,
     aggregate,
     gram_part,
-    cross_part,
     gram_in,
-    cross_in,
     gram_own,
-    cross_own,
     gram,
-    cross,
+    loss_own,
+    loss_all,
     work,
+    load_sems,
     halo_sems,
     sum_sems,
 ):
@@ -99,9 +125,32 @@
     tiles, size, feat = features_ref.shape
     rows = tiles * size
     slots = inner_ref.shape[0]
-    owners = min(total_devices, feat // 8)
-    share = feat // owners
-    own_rows = pl.ds(pl.multiple_of(lax.rem(me, owners) * share, share), share)
+    share = gram_own.shape[0]
+    owners = gram_part.shape[0] // share
+    mine = lax.div(me * owners + total_devices - 1, total_devices)
+    owns = jnp.logical_and(mine < owners, lax.div(mine * total_devices, owners) == me)
+
+    def home(owner):
+        return lax.div(owner * total_devices, owners)
+
+    def share_rows(owner):
+        return pl.ds(pl.multiple_of(owner * share, share), share)
+
+    incoming = (
+        (far_in, far_ref),
+        (near_in, near_ref),
+        (features_in, features_ref),
+        (inner_in, inner_ref),
+        (outer_in, outer_ref),
+        (dst_in, dst_ref),
+        (live_in, live_ref),
+        (tile_in, tile_ref),
+        (weight_in, weight_ref),
+    )
+    loads = [
+        pltpu.make_async_copy(source, target, load_sems.at[place])
+        for place, (source, target) in enumerate(incoming)
+    ]
 
     def device_of(index):
         return (lax.div(index, n_sub), lax.rem(index, n_sub))
@@ -112,6 +161,11 @@
     def _(offset):
         peer = lax.rem(me + offset, total_devices)
         pl.semaphore_signal(barrier, inc=1, device_id=device_of(peer), device_id_type=MESH)
+
+    for load in loads:
+        load.start()
+    for load in loads[:3]:
+        load.wait()
 
     features = features_ref[...].reshape(rows, feat)
     far_rows = jnp.dot(
@@ -191,6 +245,8 @@
             total = term if total is None else total + term
         return total
 
+    for load in loads[3:]:
+        load.wait()
     slot_products(features_ref, inner_ref, 0)
     inner_count = jnp.full((1, feat), live_ref[0, 0], jnp.int32)
     outer_count = jnp.full((1, feat), live_ref[0, 1], jnp.int32)
@@ -198,11 +254,6 @@
     @pl.loop(0, tiles)
     def _(tile):
         acc[tile] = slot_sum(tile, 0, inner_count)
-
-    features_t = features.T
-    wide = features.astype(jnp.float32)
-    square = jnp.sum(wide * wide)
-    cross_part[:, feat:] = jnp.broadcast_to(square, (feat, cross_part.shape[1] - feat))
 
     def settle(ref, sem):
         pltpu.make_async_copy(ref, ref, sem).wait()
@@ -226,93 +277,71 @@
     hidden = (
         features_ref[...].reshape(rows, feat).astype(jnp.float32) + projected / (1.0 + jnp.exp(-projected))
     ).astype(jnp.bfloat16)
-    gram_part[...] = jnp.dot(hidden.T, hidden, preferred_element_type=jnp.float32)
-
-    def scatter(part, landing, first):
-        def send(offset):
+    hidden_t = hidden.T
+    blocks = [(top, side) for top in range(0, feat, 128) for side in range(top, feat, 128)]
+    for top in range(0, feat, 128):
+        stripe = jnp.dot(
+            hidden_t[top : top + 128, :], hidden[:, top:], preferred_element_type=jnp.float32
+        )
+        for side in range(top, feat, 128):
+            at = 128 * blocks.index((top, side))
+            gram_part[at : at + 128, :] = stripe[:, side - top : side - top + 128]
+
+    @pl.loop(0, owners)
+    def _(turn):
+        owner = lax.rem(mine + turn, owners)
+        peer = home(owner)
+
+        @pl.when(peer != me)
+        def _():
+            pltpu.make_async_remote_copy(
+                src_ref=gram_part.at[share_rows(owner)],
+                dst_ref=gram_in.at[me],
+                send_sem=sum_sems.at[0],
+                recv_sem=sum_sems.at[1],
+                device_id=device_of(peer),
+                device_id_type=MESH,
+            ).start()
+
+    @pl.when(owns)
+    def _():
+        gram_in[me] = gram_part[share_rows(mine), :]
+        settle(gram_in.at[pl.ds(0, total_devices - 1)], sum_sems.at[1])
+        total = jnp.sum(gram_in[...], axis=0)
+        gram_own[...] = total
+        gram[share_rows(mine), :] = total
+
+        @pl.loop(1, total_devices)
+        def _(offset):
             peer = lax.rem(me + offset, total_devices)
-
-            def go():
-                pltpu.make_async_remote_copy(
-                    src_ref=part.at[pl.ds(pl.multiple_of(peer * share, share), share)],
-                    dst_ref=landing.at[me],
-                    send_sem=sum_sems.at[first],
-                    recv_sem=sum_sems.at[first + 1],
-                    device_id=device_of(peer),
-                    device_id_type=MESH,
-                ).start()
-
-            if owners == total_devices:
-                go()
-            else:
-                pl.when(peer < owners)(go)
-
-        pl.loop(1, total_devices)(send)
-
-    def reduce_and_gather(part, landing, own, full, first):
-        def go():
-            landing[me] = part[own_rows, :]
-            settle(landing.at[pl.ds(0, total_devices - 1)], sum_sems.at[first + 1])
-            total = jnp.sum(landing[...], axis=0)
-            own[...] = total
-            full[own_rows, :] = total
-
-            @pl.loop(1, total_devices)
-            def _(offset):
-                peer = lax.rem(me + offset, total_devices)
-                pltpu.make_async_remote_copy(
-                    src_ref=own,
-                    dst_ref=full.at[own_rows],
-                    send_sem=sum_sems.at[first + 2],
-                    recv_sem=sum_sems.at[first + 3],
-                    device_id=device_of(peer),
-                    device_id_type=MESH,
-                ).start()
-
-        if owners == total_devices:
-            go()
-        else:
-            pl.when(me < owners)(go)
-
-    def finish(part, landing, full, first):
-        def owner():
-            settle(full.at[pl.ds(0, share * (owners - 1))], sum_sems.at[first + 3])
-
-        def other():
-            settle(full, sum_sems.at[first + 3])
-
-        if owners == total_devices:
-            owner()
-        else:
-            pl.when(me < owners)(owner)
-            pl.when(me >= owners)(other)
-
-    def drain(part, landing, first):
-        def owner():
-            settle(part.at[pl.ds(0, share * (owners - 1))], sum_sems.at[first])
-            settle(landing.at[pl.ds(0, total_devices - 1)], sum_sems.at[first + 2])
-
-        def other():
-            settle(part, sum_sems.at[first])
-
-        if owners == total_devices:
-            owner()
-        else:
-            pl.when(me < owners)(owner)
-            pl.when(me >= owners)(other)
-
-    scatter(gram_part, gram_in, 0)
-    cross_part[:, :feat] = jnp.dot(features_t, hidden, preferred_element_type=jnp.float32)
-    reduce_and_gather(gram_part, gram_in, gram_own, gram, 0)
-    scatter(cross_part, cross_in, 4)
-    finish(gram_part, gram_in, gram, 0)
+            pltpu.make_async_remote_copy(
+                src_ref=gram_own,
+                dst_ref=gram.at[share_rows(mine)],
+                send_sem=sum_sems.at[2],
+                recv_sem=sum_sems.at[3],
+                device_id=device_of(peer),
+                device_id_type=MESH,
+            ).start()
+
+        settle(gram.at[pl.ds(0, share * (owners - 1))], sum_sems.at[3])
+
+    @pl.when(jnp.logical_not(owns))
+    def _():
+        settle(gram, sum_sems.at[3])
 
     vertex_count = rows * total_devices
     diagonal = lax.broadcasted_iota(jnp.int32, (feat, feat), 0) == lax.broadcasted_iota(
         jnp.int32, (feat, feat), 1
     )
     identity = jnp.where(diagonal, 1.0, 0.0)
-    work[:, :feat] = gram[...] / vertex_count + epsilon * identity
+    for top, side in blocks:
+        at = 128 * blocks.index((top, side))
+        work[top : top + 128, side : side + 128] = (
+            gram[at : at + 128, :] / vertex_count
+            + epsilon * identity[top : top + 128, side : side + 128]
+        )
+        if side > top:
+            work[side : side + 128, top : top + 128] = jnp.zeros((128, 128), jnp.float32)
     work[:, feat:] = identity
     for start in range(0, feat, LEAF):
         stop = start + LEAF
@@ -329,8 +358,6 @@
                 precision=HIGH,
                 preferred_element_type=jnp.float32,
             )
-        if start == LEAF:
-            reduce_and_gather(cross_part, cross_in, cross_own, cross, 4)
 
     lower_inverse = work[:, feat:]
     high_part = lower_inverse.astype(jnp.bfloat16)
@@ -339,20 +366,46 @@
     white = lax.dot_general(
         hidden, high_part, across, preferred_element_type=jnp.float32
     ) + lax.dot_general(hidden, low_part, across, preferred_element_type=jnp.float32)
-    out_ref[...] = white.astype(jnp.bfloat16)
-
-    whitened_gram = jnp.dot(
-        lower_inverse, gram[...], precision=HIGH, preferred_element_type=jnp.float32
-    )
-    finish(cross_part, cross_in, cross, 4)
-    distance = jnp.sum(lower_inverse * (whitened_gram - 2.0 * cross[:, :feat]))
-    square_sum = jnp.max(cross[0:8, feat:])
-    loss_ref[0, 0] = (distance + square_sum) / (vertex_count * feat)
+    result[...] = white.astype(jnp.bfloat16)
+    store = pltpu.make_async_copy(result, out_ref, load_sems.at[len(loads)])
+    store.start()
+
+    distance = white - features_ref[...].reshape(rows, feat).astype(jnp.float32)
+    wide = jnp.sum(distance * distance, axis=0, keepdims=True)
+    partial = wide[:, :128]
+    for side in range(128, feat, 128):
+        partial = partial + wide[:, side : side + 128]
+    loss_own[...] = partial
+    loss_all[me] = partial
+
+    @pl.loop(1, total_devices)
+    def _(offset):
+        peer = lax.rem(me + offset, total_devices)
+        pltpu.make_async_remote_copy(
+            src_ref=loss_own,
+            dst_ref=loss_all.at[me],
+            send_sem=sum_sems.at[4],
+            recv_sem=sum_sems.at[5],
+            device_id=device_of(peer),
+            device_id_type=MESH,
+        ).start()
 
     settle(far_send.at[pl.ds(0, per_dom * (n_dom - 1))], halo_sems.at[0])
     settle(near_send.at[pl.ds(0, per_sub * (n_sub - 1))], halo_sems.at[2])
-    drain(gram_part, gram_in, 0)
-    drain(cross_part, cross_in, 4)
+
+    @pl.when(owns)
+    def _():
+        settle(gram_part.at[pl.ds(0, share * (owners - 1))], sum_sems.at[0])
+        settle(gram_in.at[pl.ds(0, total_devices - 1)], sum_sems.at[2])
+
+    @pl.when(jnp.logical_not(owns))
+    def _():
+        settle(gram_part, sum_sems.at[0])
+
+    settle(loss_all.at[pl.ds(0, total_devices - 1)], sum_sems.at[4])
+    settle(loss_all.at[pl.ds(0, total_devices - 1)], sum_sems.at[5])
+    loss_ref[0, 0] = jnp.sum(jnp.sum(loss_all[...], axis=0)) / (vertex_count * feat)
+    store.wait()
 
 
 def body(
@@ -372,7 +425,11 @@
     size = tile_weight.shape[1]
     slots = inner_src.shape[0]
     total = n_dom * n_sub
-    share = feat // min(total, feat // 8)
+    tiles_wide = feat // 128
+    packed_rows = 128 * (tiles_wide * (tiles_wide + 1) // 2)
+    share = 8
+    while packed_rows % share or packed_rows // share > total:
+        share += 8
     far_count = send_far.shape[0]
     near_count = send_near.shape[0]
 
@@ -385,20 +442,29 @@
     near_index = padded(send_near, n_sub)
     far_padded = far_index.shape[1]
     near_padded = near_index.shape[1]
-    vmem = pl.BlockSpec(memory_space=pltpu.VMEM)
+    anywhere = pl.BlockSpec(memory_space=pl.ANY)
     smem = pl.BlockSpec(memory_space=pltpu.SMEM)
     f32 = jnp.float32
     bf16 = jnp.bfloat16
-    cross_width = feat + 128
     whitened, loss = pl.pallas_call(
         functools.partial(kernel, n_dom, n_sub, near_count // n_sub),
         out_shape=(
             jax.ShapeDtypeStruct((rows, feat), bf16),
             jax.ShapeDtypeStruct((1, 1), f32),
         ),
-        in_specs=[vmem, vmem, vmem, vmem, smem, smem, smem, smem, vmem],
-        out_specs=(vmem, smem),
+        in_specs=[anywhere] * 9,
+        out_specs=(anywhere, smem),
         scratch_shapes=[
+            pltpu.VMEM((rows // size, size, feat), bf16),
+            pltpu.VMEM(weight.shape, bf16),
+            pltpu.VMEM((1, far_padded), jnp.int32),
+            pltpu.VMEM((1, near_padded), jnp.int32),
+            pltpu.SMEM(tile_dst.shape, jnp.int32),
+            pltpu.SMEM(inner_src.shape, jnp.int32),
+            pltpu.SMEM(outer_src.shape, jnp.int32),
+            pltpu.SMEM(tile_live.shape, jnp.int32),
+            pltpu.VMEM(tile_weight.shape, bf16),
+            pltpu.VMEM((rows, feat), bf16),
             pltpu.VMEM((far_padded, feat), bf16),
             pltpu.VMEM((near_padded, feat), bf16),
             pltpu.VMEM((far_padded + near_padded, feat), bf16),
@@ -406,17 +472,16 @@
             pltpu.VMEM((slots, size, feat), f32),
             pltpu.VMEM((rows // size, size, feat), f32),
             pltpu.VMEM((rows, feat), bf16),
-            pltpu.VMEM((feat, feat), f32),
-            pltpu.VMEM((feat, cross_width), f32),
-            pltpu.VMEM((total, share, feat), f32),
-            pltpu.VMEM((total, share, cross_width), f32),
-            pltpu.VMEM((share, feat), f32),
-            pltpu.VMEM((share, cross_width), f32),
-            pltpu.VMEM((feat, feat), f32),
-            pltpu.VMEM((feat, cross_width), f32),
+            pltpu.VMEM((packed_rows, 128), f32),
+            pltpu.VMEM((total, share, 128), f32),
+            pltpu.VMEM((share, 128), f32),
+            pltpu.VMEM((packed_rows, 128), f32),
+            pltpu.VMEM((1, 128), f32),
+            pltpu.VMEM((total, 1, 128), f32),
             pltpu.VMEM((feat, 2 * feat), f32),
+            pltpu.SemaphoreType.DMA((10,)),
             pltpu.SemaphoreType.DMA((4,)),
-            pltpu.SemaphoreType.DMA((8,)),
+            pltpu.SemaphoreType.DMA((6,)),
         ],
         compiler_params=pltpu.CompilerParams(collective_id=0, has_side_effects=True),
     )(

time: 63.7 us -> 63.1 us (level)
  the two profiles are of different devices: /device:TPU:31 before, /device:TPU:0 now
where the time goes in v2:
time: 63.1 us; the launch traced here: 62.9 us
  Pallas kernels  58.7 us (93%)
  between operations  2.34 us (4%)
  local copies, waits for them, and re-layouts  1.87 us (3%)
    pallas_call x1, Pallas kernels, body(): pl.pallas_call(functools.partial(kernel, n_dom, n_sub, near_count // n_su...  58.7 us
    unnamed x1, local copies, waits for them, and re-layouts  1.87 us

profile of v2, /device:TPU:0, one launch (start us, length us, event | category | flops | bytes accessed | tf_op | source)
XLA Modules:
  0.0 62.9 jit_solution(17385481829542522899)
XLA Ops:
  0.6 58.7 %shard_map.104 = (bf16[1024,256]{1,0:T(8,128)(2,1)}, f32[1,1]{1,0:T(1,128)}) custom-call(bf16[8,128,256]{2,1,0:T(8,128)(2,1)} %bitcast.4, bf16[256,256]{1,0:T(8,128)(2,1)} %weight_in.1, s32[1,512]{1,0:T(1,128)} %bitcast.5, s32[1,128]{1,0:T(1,128)} %bitcast.6, s32[16]{0:T(128)} %dst_in.1, s32[8]{0:T(128)} %inner_in.1, s32[8]{0:T(128)} %outer_in.1, ...), custom_call_target="tpu_custom_call" | custom-call | tf_op jit(solution)/shard_map/pallas_call | solution.py:449
  59.3 1.9 %copy.13 = bf16[1024,256]{1,0:T(8,128)(2,1)} copy(bf16[1024,256]{1,0:T(8,128)(2,1)} %get-tuple-element.8) | data formatting | bytes 1048576

commit v3 on v2

--- a/solution.py
+++ b/solution.py
@@ -48,31 +48,38 @@
     row = lax.broadcasted_iota(jnp.int32, (size, size), 0)
     lane = lax.broadcasted_iota(jnp.int32, (size, size), 1)
     work = jnp.concatenate([block, jnp.where(row == lane, 1.0, 0.0)], axis=1)
-    tall = lax.broadcasted_iota(jnp.int32, (size, 1), 0)
-    for step in range(0, size - 2, 2):
-        first = work[step : step + 1, :]
-        second = work[step + 1 : step + 2, :]
-        a = first[:, step : step + 1]
-        b = first[:, step + 1 : step + 2]
-        c = second[:, step + 1 : step + 2]
-        scale = 1.0 / (a * c - b * b)
-        upper = (c * first - b * second) * scale
-        lower = (a * second - b * first) * scale
-        below = tall > step + 1
-        work = (
-            work
-            - jnp.where(below, work[:, step : step + 1], 0.0) * upper
-            - jnp.where(below, work[:, step + 1 : step + 2], 0.0) * lower
-        )
-    left = work[:, :size]
-    diagonal = jnp.sum(jnp.where(row == lane, left, 0.0), axis=1, keepdims=True)
-    before = jnp.sum(jnp.where(row == lane + 1, left, 0.0), axis=1, keepdims=True)
-    odd = lax.rem(tall, 2) == 1
-    above = pltpu.roll(jnp.broadcast_to(diagonal, (size, 2 * size)), 1, 0)
-    factor = jnp.where(odd, before, 0.0) / above
-    work = work - factor * pltpu.roll(work, 1, 0)
-    diagonal = jnp.sum(jnp.where(row == lane, work[:, :size], 0.0), axis=1, keepdims=True)
-    return work[:, size:] * (1.0 / jnp.sqrt(diagonal))
+    group = 8
+    done = []
+    for step in range(0, size, group):
+        lines = [work[i : i + 1, :] for i in range(group)]
+        entry = {
+            (i, j): jnp.broadcast_to(lines[i][:, step + j : step + j + 1], (1, 2 * size))
+            for i in range(group)
+            for j in range(i, group)
+        }
+        inverse = []
+        for i in range(group):
+            inverse.append(1.0 / entry[i, i])
+            for j in range(i + 1, group):
+                share = entry[i, j] * inverse[i]
+                for k in range(j, group):
+                    entry[j, k] = entry[j, k] - share * entry[i, k]
+                lines[j] = lines[j] - share * lines[i]
+            done.append((lines[i] / jnp.sqrt(entry[i, i]))[:, size:])
+        if step + group == size:
+            break
+        solved = [None] * group
+        for i in reversed(range(group)):
+            line = lines[i]
+            for j in range(i + 1, group):
+                line = line - entry[i, j] * solved[j]
+            solved[i] = line * inverse[i]
+        work = work[group:, :]
+        update = work[:, step : step + 1] * solved[0]
+        for i in range(1, group):
+            update = update + work[:, step + i : step + i + 1] * solved[i]
+        work = work - update
+    return jnp.concatenate(done, axis=0)
 
 
 def kernel(

time: 63.1 us -> 52.2 us (0.83)
  Pallas kernels: 58.7 us -> 47.8 us
    pallas_call x1, Pallas kernels: 58.7 us -> 47.8 us  [body(): pl.pallas_call(functools.partial(kernel, n_dom, n_sub, near_count // n_su...]
where the time goes in v3:
time: 52.2 us; the launch traced here: 52 us
  Pallas kernels  47.8 us (92%)
  between operations  2.34 us (4%)
  local copies, waits for them, and re-layouts  1.87 us (4%)
    pallas_call x1, Pallas kernels, body(): pl.pallas_call(functools.partial(kernel, n_dom, n_sub, near_count // n_su...  47.8 us
    unnamed x1, local copies, waits for them, and re-layouts  1.87 us

profile of v3, /device:TPU:0, one launch (start us, length us, event | category | flops | bytes accessed | tf_op | source)
XLA Modules:
  0.0 52.0 jit_solution(14589403341662787308)
XLA Ops:
  0.6 47.8 %shard_map.104 = (bf16[1024,256]{1,0:T(8,128)(2,1)}, f32[1,1]{1,0:T(1,128)}) custom-call(bf16[8,128,256]{2,1,0:T(8,128)(2,1)} %bitcast.4, bf16[256,256]{1,0:T(8,128)(2,1)} %weight_in.1, s32[1,512]{1,0:T(1,128)} %bitcast.5, s32[1,128]{1,0:T(1,128)} %bitcast.6, s32[16]{0:T(128)} %dst_in.1, s32[8]{0:T(128)} %inner_in.1, s32[8]{0:T(128)} %outer_in.1, ...), custom_call_target="tpu_custom_call" | custom-call | tf_op jit(solution)/shard_map/pallas_call | solution.py:456
  48.5 1.9 %copy.13 = bf16[1024,256]{1,0:T(8,128)(2,1)} copy(bf16[1024,256]{1,0:T(8,128)(2,1)} %get-tuple-element.8) | data formatting | bytes 1048576
